TPU v7x, 128 devices: a whole 4x4x4 slice. The times are simulated.
128 devices in a mesh: sec: 64 (over x, y, z), node: 2 (over core).
Axes of the slice: x: 4, y: 4, z: 4, core: 2. Of those that a mesh axis runs over, the one named last changes fastest.
Arguments:
- env_blocks: bfloat16 [2, 24576, 128, 128], P('node', 'sec'), may hold values from -10 to 10, as said below
- iso_blocks: bfloat16 [2, 24576, 128, 128], P('node', 'sec'), may hold values from -6 to 6
- joined_sector: int32 [2, 24576], P('node', 'sec'), may hold values from 0 to 63, as said below
- owner_map: int32 [2, 64], P('node'), may hold values from 0 to 63, each once within a row
- live_pairs: int32 [2, 64], P('node', 'sec'), may hold values from 1 to 384, as said below
Outputs:
- environment: float32 [2, 64, 128, 128], P('node', 'sec')
Inputs may be any that keep to these rules, and one draw needn't show every extreme that they name: `env_blocks`: each block is symmetric. `joined_sector`: slot p belongs to tree node k = p // 3072 of its group, and its sector is one of that node's sectors k * 8 to k * 8 + 7. `owner_map`: each row names every index once. `live_pairs`: in every group some index of sec has all 384 slots live.
All inputs are finite; a program needn't handle non-finite values.
Results may differ from a plain program's by a relative error of at most 0.0003.
Values sent between devices are 32-bit elements; how exact they have to be, the bound alone decides.
A program may use at most 128 MiB of HBM per device.

v0:
```python
import jax
import jax.numpy as jnp
from jax import lax
from jax.sharding import Mesh
from jax.sharding import PartitionSpec as P

SEC = ("sec_0", "sec_1", "sec_2")
SEC_NODE = ("sec_0", "sec_1", "sec_2", "node")
pair_group = 32


def cut_along(shard, dim, length):
    shape = shard.shape
    blocks = shard.reshape(*shape[:dim], length, shape[dim] // length, *shape[dim + 1 :])
    return jnp.moveaxis(blocks, dim, 0)


def sum_at_owner(shard, axis, dim):
    length = lax.axis_size(axis)
    blocks = lax.all_to_all(cut_along(shard, dim, length), axis, 0, 0, tiled=True)
    return jnp.sum(blocks, axis=0)


def by_axis(shard, axes):
    for axis in axes:
        shard = lax.psum(shard, axis)
    return shard


def body(env_blocks, iso_blocks, joined_sector, owner_map, live_pairs):
    pairs_here = env_blocks.shape[1]
    sector_width = iso_blocks.shape[3]
    half_width = sector_width // 2
    sectors = lax.axis_size(SEC)
    sector_ids = jnp.arange(sectors, dtype=jnp.int32)
    matches = joined_sector[0][:, None] == sector_ids[None, :]
    targets = jnp.sum(jnp.where(matches, owner_map[0][None, :], 0), axis=1)
    living = jnp.arange(pairs_here, dtype=jnp.int32) < live_pairs[0, 0]

    def add_group(turn_index, partial_value):
        first_pair = turn_index * pair_group
        blocks = lax.dynamic_slice_in_dim(env_blocks[0], first_pair, pair_group, 0)
        weights = lax.dynamic_slice_in_dim(iso_blocks[0], first_pair, pair_group, 0)
        group_targets = lax.dynamic_slice_in_dim(targets, first_pair, pair_group, 0)
        group_live = lax.dynamic_slice_in_dim(living, first_pair, pair_group, 0)
        product = jnp.einsum(
            "prk,pkc->prc", blocks, weights, preferred_element_type=jnp.float32
        ).astype(jnp.bfloat16)
        sandwich = jnp.einsum("prc,prd->pcd", weights, product, preferred_element_type=jnp.float32)
        selector = ((group_targets[:, None] == sector_ids[None, :]) & group_live[:, None]).astype(
            jnp.float32
        )
        flat_terms = sandwich.reshape(pair_group, sector_width * sector_width)
        added = lax.dot_general(
            selector,
            flat_terms,
            (((0,), (0,)), ((), ())),
            precision=lax.Precision.HIGHEST,
            preferred_element_type=jnp.float32,
        )
        return partial_value + added

    zero_sums = jnp.zeros((sectors, sector_width * sector_width), jnp.float32)
    turn_total = pairs_here // pair_group
    partial_value = lax.fori_loop(0, turn_total, add_group, zero_sums).reshape(
        sectors, sector_width, sector_width
    )
    upper_left = partial_value[:, :half_width, :half_width]
    upper_right = partial_value[:, :half_width, half_width:]
    lower_right = partial_value[:, half_width:, half_width:]
    corners = jnp.triu(upper_left) + jnp.tril(jnp.swapaxes(lower_right, 1, 2), -1)
    diagonal_row = jnp.diagonal(lower_right, axis1=1, axis2=2)[:, None, :]
    packed = jnp.concatenate((corners, upper_right, diagonal_row), axis=1)
    summed = sum_at_owner(packed, SEC, 0)[0]
    corners_sum = summed[:half_width]
    right_sum = summed[half_width : 2 * half_width]
    diagonal_sum = summed[2 * half_width]
    left_block = jnp.triu(corners_sum) + jnp.triu(corners_sum, 1).T
    lower_upper = jnp.tril(corners_sum, -1).T + jnp.diag(diagonal_sum)
    right_block = lower_upper + jnp.triu(lower_upper, 1).T
    top_rows = jnp.concatenate((left_block, right_sum), axis=1)
    bottom_rows = jnp.concatenate((right_sum.T, right_block), axis=1)
    hermitian = jnp.concatenate((top_rows, bottom_rows), axis=0)
    squares = jnp.sum(hermitian * hermitian)
    grand_total = by_axis(squares, SEC_NODE)
    entries = sectors * lax.axis_size("node") * sector_width * sector_width
    factor = lax.rsqrt(grand_total / entries + 1e-06)
    return (hermitian * factor)[None, None]


def solution(mesh):
    split = Mesh(
        mesh.devices.reshape(4, 4, 4, mesh.shape["node"]), ("sec_0", "sec_1", "sec_2", "node")
    )
    placed = (
        P("node", SEC, None, None),
        P("node", SEC, None, None),
        P("node", SEC),
        P("node", None),
        P("node", SEC),
    )
    return jax.shard_map(
        body, mesh=split, in_specs=placed, out_specs=P("node", SEC, None, None), check_vma=False
    )
```

profile of v0, /device:TPU:1, one launch (start us, length us, event | category | flops | bytes accessed | tf_op | source)
XLA Modules:
  0.0 255.1 jit_solution(2081290549324022647)
XLA Ops:
  2.1 121.4 %while.14 = (s32[]{:T(128)}, f32[64,16384]{1,0:T(8,128)}, s32[384]{0:T(512)S(1)}, pred[384]{0:T(512)(128)(4,1)S(1)}, bf16[1,384,128,128]{3,2,1,0:T(8,128)(2,1)},...) while((s32[]{:T(128)}, f32[64,16384]{1,0:T(8,128)}, ...), condition=%wide.region_2.3_spmd.clone, body=%wide.region_1.2_spmd.clone.sunk | while | flops 673714176 | bytes 15730821 | solution.py:65
  2.1 2.6 %fusion.36 = f32[32,128,128]{2,1,0:T(8,128)S(1)} fusion(bf16[1,384,128,128]{3,2,1,0:T(8,128)(2,1)} %get-tuple-element.248, s32[]{:T(128)S(6)} %select_n.72, bf16[1,384,128,128]{3,2,1,0:T(8,128)(2,1)} %get-tuple-element.247), kind=kOutput, calls=%fused_computation.6.clone.1 | convolution fusion | flops 268959744 | bytes 5244416 | tf_op jit(solution)/shard_map/while/body/eval_jaxpr/prc,prd->pcd/dot_general | solution.py:49
  4.9 5.3 %convolution_add_fusion.2 = f32[64,16384]{1,0:T(8,128)} fusion(f32[64,16384]{1,0:T(8,128)} %get-tuple-element.234, f32[4,8,128,128]{3,2,1,0:T(8,128)S(1)} %bitcast.64, pred[]{:T(512)S(6)} %compare.3, s32[32]{0:T(128)S(1)} %dynamic_slice.54, pred[32]{0:T(512)(128)(4,1)S(1)} %dynamic_slice.55), kind=kOutput, calls=%fused_computation.2.clone.1 | convolution fusion | flops 404754432 | bytes 10485921 | tf_op jit(solution)/shard_map/while/body/eval_jaxpr/dot_general | solution.py:54
  10.2 2.6 %fusion.36 = f32[32,128,128]{2,1,0:T(8,128)S(1)} fusion(bf16[1,384,128,128]{3,2,1,0:T(8,128)(2,1)} %get-tuple-element.248, s32[]{:T(128)S(6)} %select_n.72, bf16[1,384,128,128]{3,2,1,0:T(8,128)(2,1)} %get-tuple-element.247), kind=kOutput, calls=%fused_computation.6.clone.1 | convolution fusion | flops 268959744 | bytes 5244416 | tf_op jit(solution)/shard_map/while/body/eval_jaxpr/prc,prd->pcd/dot_general | solution.py:49
  13.0 7.5 %convolution_add_fusion.2 = f32[64,16384]{1,0:T(8,128)} fusion(f32[64,16384]{1,0:T(8,128)} %get-tuple-element.234, f32[4,8,128,128]{3,2,1,0:T(8,128)S(1)} %bitcast.64, pred[]{:T(512)S(6)} %compare.3, s32[32]{0:T(128)S(1)} %dynamic_slice.54, pred[32]{0:T(512)(128)(4,1)S(1)} %dynamic_slice.55), kind=kOutput, calls=%fused_computation.2.clone.1 | convolution fusion | flops 404754432 | bytes 10485921 | tf_op jit(solution)/shard_map/while/body/eval_jaxpr/dot_general | solution.py:54
  20.5 2.6 %fusion.36 = f32[32,128,128]{2,1,0:T(8,128)S(1)} fusion(bf16[1,384,128,128]{3,2,1,0:T(8,128)(2,1)} %get-tuple-element.248, s32[]{:T(128)S(6)} %select_n.72, bf16[1,384,128,128]{3,2,1,0:T(8,128)(2,1)} %get-tuple-element.247), kind=kOutput, calls=%fused_computation.6.clone.1 | convolution fusion | flops 268959744 | bytes 5244416 | tf_op jit(solution)/shard_map/while/body/eval_jaxpr/prc,prd->pcd/dot_general | solution.py:49
  23.3 7.5 %convolution_add_fusion.2 = f32[64,16384]{1,0:T(8,128)} fusion(f32[64,16384]{1,0:T(8,128)} %get-tuple-element.234, f32[4,8,128,128]{3,2,1,0:T(8,128)S(1)} %bitcast.64, pred[]{:T(512)S(6)} %compare.3, s32[32]{0:T(128)S(1)} %dynamic_slice.54, pred[32]{0:T(512)(128)(4,1)S(1)} %dynamic_slice.55), kind=kOutput, calls=%fused_computation.2.clone.1 | convolution fusion | flops 404754432 | bytes 10485921 | tf_op jit(solution)/shard_map/while/body/eval_jaxpr/dot_general | solution.py:54
  30.8 2.6 %fusion.36 = f32[32,128,128]{2,1,0:T(8,128)S(1)} fusion(bf16[1,384,128,128]{3,2,1,0:T(8,128)(2,1)} %get-tuple-element.248, s32[]{:T(128)S(6)} %select_n.72, bf16[1,384,128,128]{3,2,1,0:T(8,128)(2,1)} %get-tuple-element.247), kind=kOutput, calls=%fused_computation.6.clone.1 | convolution fusion | flops 268959744 | bytes 5244416 | tf_op jit(solution)/shard_map/while/body/eval_jaxpr/prc,prd->pcd/dot_general | solution.py:49
  33.5 7.5 %convolution_add_fusion.2 = f32[64,16384]{1,0:T(8,128)} fusion(f32[64,16384]{1,0:T(8,128)} %get-tuple-element.234, f32[4,8,128,128]{3,2,1,0:T(8,128)S(1)} %bitcast.64, pred[]{:T(512)S(6)} %compare.3, s32[32]{0:T(128)S(1)} %dynamic_slice.54, pred[32]{0:T(512)(128)(4,1)S(1)} %dynamic_slice.55), kind=kOutput, calls=%fused_computation.2.clone.1 | convolution fusion | flops 404754432 | bytes 10485921 | tf_op jit(solution)/shard_map/while/body/eval_jaxpr/dot_general | solution.py:54
  43.8 7.5 %convolution_add_fusion.2 = f32[64,16384]{1,0:T(8,128)} fusion(f32[64,16384]{1,0:T(8,128)} %get-tuple-element.234, f32[4,8,128,128]{3,2,1,0:T(8,128)S(1)} %bitcast.64, pred[]{:T(512)S(6)} %compare.3, s32[32]{0:T(128)S(1)} %dynamic_slice.54, pred[32]{0:T(512)(128)(4,1)S(1)} %dynamic_slice.55), kind=kOutput, calls=%fused_computation.2.clone.1 | convolution fusion | flops 404754432 | bytes 10485921 | tf_op jit(solution)/shard_map/while/body/eval_jaxpr/dot_general | solution.py:54
  51.3 2.6 %fusion.36 = f32[32,128,128]{2,1,0:T(8,128)S(1)} fusion(bf16[1,384,128,128]{3,2,1,0:T(8,128)(2,1)} %get-tuple-element.248, s32[]{:T(128)S(6)} %select_n.72, bf16[1,384,128,128]{3,2,1,0:T(8,128)(2,1)} %get-tuple-element.247), kind=kOutput, calls=%fused_computation.6.clone.1 | convolution fusion | flops 268959744 | bytes 5244416 | tf_op jit(solution)/shard_map/while/body/eval_jaxpr/prc,prd->pcd/dot_general | solution.py:49
  54.1 7.5 %convolution_add_fusion.2 = f32[64,16384]{1,0:T(8,128)} fusion(f32[64,16384]{1,0:T(8,128)} %get-tuple-element.234, f32[4,8,128,128]{3,2,1,0:T(8,128)S(1)} %bitcast.64, pred[]{:T(512)S(6)} %compare.3, s32[32]{0:T(128)S(1)} %dynamic_slice.54, pred[32]{0:T(512)(128)(4,1)S(1)} %dynamic_slice.55), kind=kOutput, calls=%fused_computation.2.clone.1 | convolution fusion | flops 404754432 | bytes 10485921 | tf_op jit(solution)/shard_map/while/body/eval_jaxpr/dot_general | solution.py:54
  61.6 2.8 %fusion.36 = f32[32,128,128]{2,1,0:T(8,128)S(1)} fusion(bf16[1,384,128,128]{3,2,1,0:T(8,128)(2,1)} %get-tuple-element.248, s32[]{:T(128)S(6)} %select_n.72, bf16[1,384,128,128]{3,2,1,0:T(8,128)(2,1)} %get-tuple-element.247), kind=kOutput, calls=%fused_computation.6.clone.1 | convolution fusion | flops 268959744 | bytes 5244416 | tf_op jit(solution)/shard_map/while/body/eval_jaxpr/prc,prd->pcd/dot_general | solution.py:49
  64.6 7.5 %convolution_add_fusion.2 = f32[64,16384]{1,0:T(8,128)} fusion(f32[64,16384]{1,0:T(8,128)} %get-tuple-element.234, f32[4,8,128,128]{3,2,1,0:T(8,128)S(1)} %bitcast.64, pred[]{:T(512)S(6)} %compare.3, s32[32]{0:T(128)S(1)} %dynamic_slice.54, pred[32]{0:T(512)(128)(4,1)S(1)} %dynamic_slice.55), kind=kOutput, calls=%fused_computation.2.clone.1 | convolution fusion | flops 404754432 | bytes 10485921 | tf_op jit(solution)/shard_map/while/body/eval_jaxpr/dot_general | solution.py:54
  72.1 2.6 %fusion.36 = f32[32,128,128]{2,1,0:T(8,128)S(1)} fusion(bf16[1,384,128,128]{3,2,1,0:T(8,128)(2,1)} %get-tuple-element.248, s32[]{:T(128)S(6)} %select_n.72, bf16[1,384,128,128]{3,2,1,0:T(8,128)(2,1)} %get-tuple-element.247), kind=kOutput, calls=%fused_computation.6.clone.1 | convolution fusion | flops 268959744 | bytes 5244416 | tf_op jit(solution)/shard_map/while/body/eval_jaxpr/prc,prd->pcd/dot_general | solution.py:49
  74.9 7.5 %convolution_add_fusion.2 = f32[64,16384]{1,0:T(8,128)} fusion(f32[64,16384]{1,0:T(8,128)} %get-tuple-element.234, f32[4,8,128,128]{3,2,1,0:T(8,128)S(1)} %bitcast.64, pred[]{:T(512)S(6)} %compare.3, s32[32]{0:T(128)S(1)} %dynamic_slice.54, pred[32]{0:T(512)(128)(4,1)S(1)} %dynamic_slice.55), kind=kOutput, calls=%fused_computation.2.clone.1 | convolution fusion | flops 404754432 | bytes 10485921 | tf_op jit(solution)/shard_map/while/body/eval_jaxpr/dot_general | solution.py:54
  85.2 7.5 %convolution_add_fusion.2 = f32[64,16384]{1,0:T(8,128)} fusion(f32[64,16384]{1,0:T(8,128)} %get-tuple-element.234, f32[4,8,128,128]{3,2,1,0:T(8,128)S(1)} %bitcast.64, pred[]{:T(512)S(6)} %compare.3, s32[32]{0:T(128)S(1)} %dynamic_slice.54, pred[32]{0:T(512)(128)(4,1)S(1)} %dynamic_slice.55), kind=kOutput, calls=%fused_computation.2.clone.1 | convolution fusion | flops 404754432 | bytes 10485921 | tf_op jit(solution)/shard_map/while/body/eval_jaxpr/dot_general | solution.py:54
  95.4 7.5 %convolution_add_fusion.2 = f32[64,16384]{1,0:T(8,128)} fusion(f32[64,16384]{1,0:T(8,128)} %get-tuple-element.234, f32[4,8,128,128]{3,2,1,0:T(8,128)S(1)} %bitcast.64, pred[]{:T(512)S(6)} %compare.3, s32[32]{0:T(128)S(1)} %dynamic_slice.54, pred[32]{0:T(512)(128)(4,1)S(1)} %dynamic_slice.55), kind=kOutput, calls=%fused_computation.2.clone.1 | convolution fusion | flops 404754432 | bytes 10485921 | tf_op jit(solution)/shard_map/while/body/eval_jaxpr/dot_general | solution.py:54
  102.9 2.7 %fusion.36 = f32[32,128,128]{2,1,0:T(8,128)S(1)} fusion(bf16[1,384,128,128]{3,2,1,0:T(8,128)(2,1)} %get-tuple-element.248, s32[]{:T(128)S(6)} %select_n.72, bf16[1,384,128,128]{3,2,1,0:T(8,128)(2,1)} %get-tuple-element.247), kind=kOutput, calls=%fused_computation.6.clone.1 | convolution fusion | flops 268959744 | bytes 5244416 | tf_op jit(solution)/shard_map/while/body/eval_jaxpr/prc,prd->pcd/dot_general | solution.py:49
  105.8 7.5 %convolution_add_fusion.2 = f32[64,16384]{1,0:T(8,128)} fusion(f32[64,16384]{1,0:T(8,128)} %get-tuple-element.234, f32[4,8,128,128]{3,2,1,0:T(8,128)S(1)} %bitcast.64, pred[]{:T(512)S(6)} %compare.3, s32[32]{0:T(128)S(1)} %dynamic_slice.54, pred[32]{0:T(512)(128)(4,1)S(1)} %dynamic_slice.55), kind=kOutput, calls=%fused_computation.2.clone.1 | convolution fusion | flops 404754432 | bytes 10485921 | tf_op jit(solution)/shard_map/while/body/eval_jaxpr/dot_general | solution.py:54
  113.3 2.6 %fusion.36 = f32[32,128,128]{2,1,0:T(8,128)S(1)} fusion(bf16[1,384,128,128]{3,2,1,0:T(8,128)(2,1)} %get-tuple-element.248, s32[]{:T(128)S(6)} %select_n.72, bf16[1,384,128,128]{3,2,1,0:T(8,128)(2,1)} %get-tuple-element.247), kind=kOutput, calls=%fused_computation.6.clone.1 | convolution fusion | flops 268959744 | bytes 5244416 | tf_op jit(solution)/shard_map/while/body/eval_jaxpr/prc,prd->pcd/dot_general | solution.py:49
  116.1 7.5 %convolution_add_fusion.2 = f32[64,16384]{1,0:T(8,128)} fusion(f32[64,16384]{1,0:T(8,128)} %get-tuple-element.234, f32[4,8,128,128]{3,2,1,0:T(8,128)S(1)} %bitcast.64, pred[]{:T(512)S(6)} %compare.3, s32[32]{0:T(128)S(1)} %dynamic_slice.54, pred[32]{0:T(512)(128)(4,1)S(1)} %dynamic_slice.55), kind=kOutput, calls=%fused_computation.2.clone.1 | convolution fusion | flops 404754432 | bytes 10485921 | tf_op jit(solution)/shard_map/while/body/eval_jaxpr/dot_general | solution.py:54
  123.6 2.9 %copy.65 = f32[8,8,128,128]{3,2,1,0:T(8,128)S(1)} copy(f32[8,8,128,128]{3,1,2,0:T(8,128)} %bitcast.65) | data formatting | bytes 8388608
  126.5 3.8 %fusion.24 = (f32[64,64,64]{2,1,0:T(8,128)}, f32[64,64,64]{2,1,0:T(8,128)}, f32[64,64,64]{2,1,0:T(8,128)}) fusion(f32[64,128,128]{2,1,0:T(8,128)S(1)} %bitcast.66), kind=kLoop, calls=%fused_computation.43 | loop fusion | bytes 6291456 | tf_op jit(solution)/shard_map/slice | solution.py:68
  132.7 4.2 %copy.61 = f32[64,64,64]{0,1,2:T(8,128)} copy(f32[64,64,64]{2,1,0:T(8,128)} %get-tuple-element.177) | data formatting | bytes 2097152
  136.8 4.2 %copy.63 = f32[64,64,64]{0,1,2:T(8,128)} copy(f32[64,64,64]{2,1,0:T(8,128)} %get-tuple-element.178) | data formatting | bytes 2097152
  146.5 6.4 %copy.53 = f32[64,1,129,64]{2,3,1,0:T(8,128)} copy(f32[64,1,129,64]{0,2,3,1:T(8,128)} %maximum_bitcast_fusion) | data formatting | bytes 4227072 | tf_op jit(solution)/shard_map/reshape | solution.py:14
  152.9 62.3 %all_to_all.5 = f32[64,1,129,64]{2,3,1,0:T(8,128)} all-to-all(f32[64,1,129,64]{2,3,1,0:T(8,128)} %copy.53), channel_id=1, replica_groups=mesh['sec_0'=4,'sec_1'=4,'sec_2'=4,'node'=2] {'sec_0','sec_1','sec_2'}, dimensions={0} | all-to-all | bytes 4227072 | tf_op jit(solution)/shard_map/all_to_all | solution.py:20
  219.0 7.3 %psum.28 = f32[]{:T(128)} all-reduce(f32[]{:T(128)} %fusion.20), channel_id=1, replica_groups=mesh['sec_0'=4,'sec_1'=4,'sec_2'=4,'node'=2] {'sec_0'}, use_global_device_ids=true, to_apply=%region_5.6 | all-reduce | flops 1 | bytes 8 | tf_op jit(solution)/shard_map/psum | solution.py:26
  226.3 10.5 %psum.29 = f32[]{:T(128)} all-reduce(f32[]{:T(128)} %psum.28), channel_id=1, replica_groups=mesh['sec_0'=4,'sec_1'=4,'sec_2'=4,'node'=2] {'sec_1'}, use_global_device_ids=true, to_apply=%region_6.7 | all-reduce | flops 1 | bytes 8 | tf_op jit(solution)/shard_map/psum | solution.py:26
  236.8 7.6 %psum.30 = f32[]{:T(128)} all-reduce(f32[]{:T(128)} %psum.29), channel_id=1, replica_groups=mesh['sec_0'=4,'sec_1'=4,'sec_2'=4,'node'=2] {'sec_2'}, use_global_device_ids=true, to_apply=%region_7.8 | all-reduce | flops 1 | bytes 8 | tf_op jit(solution)/shard_map/psum | solution.py:26
  244.5 9.3 %psum.31 = f32[]{:T(128)} all-reduce(f32[]{:T(128)} %psum.30), channel_id=1, replica_groups=mesh['sec_0'=4,'sec_1'=4,'sec_2'=4,'node'=2] {'node'}, use_global_device_ids=true, to_apply=%region_8.9 | all-reduce | flops 1 | bytes 8 | tf_op jit(solution)/shard_map/psum | solution.py:26
  (53 shorter events, 23.5 us)
Async XLA Ops:
  141.9 2.2 copy-start
where the time goes:
time: 256 us; the launch traced here: 255 us
  matrix products  119 us (46%)
  blocking collectives  97 us (38%)
  local copies, waits for them, and re-layouts  27.1 us (11%)
  other arithmetic  10 us (4%)
    dot_general x12, matrix products, add_group(): lax.dot_general(selector, flat_terms, (((0,), (0,)), ((), ())), precision...  87.8 us
    all_to_all x1, blocking collectives, sum_at_owner(): lax.all_to_all(cut_along(shard, dim, length), axis, 0, 0, tiled=True)  62.3 us
    psum x4, blocking collectives, by_axis(): shard = lax.psum(shard, axis)  34.7 us
    dot_general x12, matrix products, add_group(): jnp.einsum('prc,prd->pcd', weights, product, preferred_element_type=jnp.f...  31.6 us
    unnamed x6, local copies, waits for them, and re-layouts  13.7 us
    reshape x1, local copies, waits for them, and re-layouts, cut_along(): shard.reshape(*shape[:dim], length, shape[dim] // length, *shape[dim + 1:])  6.38 us

commit v1 on v0

--- a/solution.py
+++ b/solution.py
@@ -23,7 +23,8 @@
 
 def by_axis(shard, axes):
     for axis in axes:
-        shard = lax.psum(shard, axis)
+        parts = lax.all_gather(shard, axis)
+        shard = jnp.sum(parts, axis=0)
     return shard
 
 

time: 256 us -> 269 us (1.051)
  blocking collectives: 97 us -> 35.4 us
  waiting for transfers between devices: 0 us -> 50.7 us
  starting transfers between devices: 0 us -> 12.3 us
  local copies, waits for them, and re-layouts: 27.1 us -> 35.4 us
    all_to_all x1 -> x0, blocking collectives: 62.3 us -> none  [sum_at_owner(): lax.all_to_all(cut_along(shard, dim, length), axis, 0, 0, tiled=True)]
    all_to_all x0 -> x1, waiting for transfers between devices: none -> 50.7 us  [sum_at_owner(): lax.all_to_all(cut_along(shard, dim, length), axis, 0, 0, tiled=True)]
    unnamed x0 -> x4, blocking collectives: none -> 35.4 us
    psum x4 -> x0, blocking collectives: 34.7 us -> none  [by_axis(): shard = lax.psum(shard, axis)]
    all_to_all x0 -> x1, starting transfers between devices: none -> 12.3 us  [sum_at_owner(): lax.all_to_all(cut_along(shard, dim, length), axis, 0, 0, tiled=True)]
    unnamed x6 -> x26, local copies, waits for them, and re-layouts: 13.7 us -> 22 us
  transfers between devices with their start and end apart: 0 -> 1, of which waited for: 0 -> 1; matrix products, arithmetic and copies ran while one was open for 0% -> 0% of each run, Pallas kernels for 0% -> 0%
where the time goes in v1:
time: 269 us; the launch traced here: 267 us
  matrix products  119 us (44%)
  waiting for transfers between devices  50.7 us (19%)
  local copies, waits for them, and re-layouts  35.4 us (13%)
  blocking collectives  35.4 us (13%)
  other arithmetic  12.4 us (5%)
  starting transfers between devices  12.3 us (5%)
    dot_general x12, matrix products, add_group(): lax.dot_general(selector, flat_terms, (((0,), (0,)), ((), ())), precision...  87.8 us
    all_to_all x1, waiting for transfers between devices, sum_at_owner(): lax.all_to_all(cut_along(shard, dim, length), axis, 0, 0, tiled=True)  50.7 us
    unnamed x4, blocking collectives  35.4 us
    dot_general x12, matrix products, add_group(): jnp.einsum('prc,prd->pcd', weights, product, preferred_element_type=jnp.f...  31.6 us
    unnamed x26, local copies, waits for them, and re-layouts  22 us
    all_to_all x1, starting transfers between devices, sum_at_owner(): lax.all_to_all(cut_along(shard, dim, length), axis, 0, 0, tiled=True)  12.3 us
    reshape x1, local copies, waits for them, and re-layouts, cut_along(): shard.reshape(*shape[:dim], length, shape[dim] // length, *shape[dim + 1:])  6.38 us
  transfers between devices with their start and end apart: 1, of which 1 were waited for; matrix products, arithmetic and copies ran while one was open for 0% of the time, Pallas kernels for 0%

profile of v1, /device:TPU:1, one launch (start us, length us, event | category | flops | bytes accessed | tf_op | source)
XLA Modules:
  0.0 267.4 jit_solution(6140445280505164742)
XLA Ops:
  2.1 121.4 %while.14 = (s32[]{:T(128)}, f32[64,16384]{1,0:T(8,128)}, s32[384]{0:T(512)S(1)}, pred[384]{0:T(512)(128)(4,1)S(1)}, bf16[1,384,128,128]{3,2,1,0:T(8,128)(2,1)},...) while((s32[]{:T(128)}, f32[64,16384]{1,0:T(8,128)}, ...), condition=%wide.region_2.3_spmd.clone, body=%wide.region_1.2_spmd.clone.sunk | while | flops 673714176 | bytes 15730821 | solution.py:66
  2.1 2.6 fusion.36
  4.9 5.3 %convolution_add_fusion.2 = f32[64,16384]{1,0:T(8,128)} fusion(f32[64,16384]{1,0:T(8,128)} %get-tuple-element.234, f32[4,8,128,128]{3,2,1,0:T(8,128)S(1)} %bitcast.72, pred[]{:T(512)S(6)} %compare.3, s32[32]{0:T(128)S(1)} %dynamic_slice.54, pred[32]{0:T(512)(128)(4,1)S(1)} %dynamic_slice.55), kind=kOutput, calls=%fused_computation.2.clone.1 | convolution fusion | flops 404754432 | bytes 10485921 | tf_op jit(solution)/shard_map/while/body/eval_jaxpr/dot_general | solution.py:55
  10.2 2.6 fusion.36
  13.0 7.5 %convolution_add_fusion.2 = f32[64,16384]{1,0:T(8,128)} fusion(f32[64,16384]{1,0:T(8,128)} %get-tuple-element.234, f32[4,8,128,128]{3,2,1,0:T(8,128)S(1)} %bitcast.72, pred[]{:T(512)S(6)} %compare.3, s32[32]{0:T(128)S(1)} %dynamic_slice.54, pred[32]{0:T(512)(128)(4,1)S(1)} %dynamic_slice.55), kind=kOutput, calls=%fused_computation.2.clone.1 | convolution fusion | flops 404754432 | bytes 10485921 | tf_op jit(solution)/shard_map/while/body/eval_jaxpr/dot_general | solution.py:55
  20.5 2.6 fusion.36
  23.3 7.5 %convolution_add_fusion.2 = f32[64,16384]{1,0:T(8,128)} fusion(f32[64,16384]{1,0:T(8,128)} %get-tuple-element.234, f32[4,8,128,128]{3,2,1,0:T(8,128)S(1)} %bitcast.72, pred[]{:T(512)S(6)} %compare.3, s32[32]{0:T(128)S(1)} %dynamic_slice.54, pred[32]{0:T(512)(128)(4,1)S(1)} %dynamic_slice.55), kind=kOutput, calls=%fused_computation.2.clone.1 | convolution fusion | flops 404754432 | bytes 10485921 | tf_op jit(solution)/shard_map/while/body/eval_jaxpr/dot_general | solution.py:55
  33.5 7.5 %convolution_add_fusion.2 = f32[64,16384]{1,0:T(8,128)} fusion(f32[64,16384]{1,0:T(8,128)} %get-tuple-element.234, f32[4,8,128,128]{3,2,1,0:T(8,128)S(1)} %bitcast.72, pred[]{:T(512)S(6)} %compare.3, s32[32]{0:T(128)S(1)} %dynamic_slice.54, pred[32]{0:T(512)(128)(4,1)S(1)} %dynamic_slice.55), kind=kOutput, calls=%fused_computation.2.clone.1 | convolution fusion | flops 404754432 | bytes 10485921 | tf_op jit(solution)/shard_map/while/body/eval_jaxpr/dot_general | solution.py:55
  43.8 7.5 %convolution_add_fusion.2 = f32[64,16384]{1,0:T(8,128)} fusion(f32[64,16384]{1,0:T(8,128)} %get-tuple-element.234, f32[4,8,128,128]{3,2,1,0:T(8,128)S(1)} %bitcast.72, pred[]{:T(512)S(6)} %compare.3, s32[32]{0:T(128)S(1)} %dynamic_slice.54, pred[32]{0:T(512)(128)(4,1)S(1)} %dynamic_slice.55), kind=kOutput, calls=%fused_computation.2.clone.1 | convolution fusion | flops 404754432 | bytes 10485921 | tf_op jit(solution)/shard_map/while/body/eval_jaxpr/dot_general | solution.py:55
  51.3 2.6 fusion.36
  54.1 7.5 %convolution_add_fusion.2 = f32[64,16384]{1,0:T(8,128)} fusion(f32[64,16384]{1,0:T(8,128)} %get-tuple-element.234, f32[4,8,128,128]{3,2,1,0:T(8,128)S(1)} %bitcast.72, pred[]{:T(512)S(6)} %compare.3, s32[32]{0:T(128)S(1)} %dynamic_slice.54, pred[32]{0:T(512)(128)(4,1)S(1)} %dynamic_slice.55), kind=kOutput, calls=%fused_computation.2.clone.1 | convolution fusion | flops 404754432 | bytes 10485921 | tf_op jit(solution)/shard_map/while/body/eval_jaxpr/dot_general | solution.py:55
  61.6 2.8 %fusion.36 = f32[32,128,128]{2,1,0:T(8,128)S(1)} fusion(bf16[1,384,128,128]{3,2,1,0:T(8,128)(2,1)} %get-tuple-element.248, s32[]{:T(128)S(6)} %select_n.72, bf16[1,384,128,128]{3,2,1,0:T(8,128)(2,1)} %get-tuple-element.247), kind=kOutput, calls=%fused_computation.6.clone.1 | convolution fusion | flops 268959744 | bytes 5244416 | tf_op jit(solution)/shard_map/while/body/eval_jaxpr/prc,prd->pcd/dot_general | solution.py:50
  64.6 7.5 %convolution_add_fusion.2 = f32[64,16384]{1,0:T(8,128)} fusion(f32[64,16384]{1,0:T(8,128)} %get-tuple-element.234, f32[4,8,128,128]{3,2,1,0:T(8,128)S(1)} %bitcast.72, pred[]{:T(512)S(6)} %compare.3, s32[32]{0:T(128)S(1)} %dynamic_slice.54, pred[32]{0:T(512)(128)(4,1)S(1)} %dynamic_slice.55), kind=kOutput, calls=%fused_computation.2.clone.1 | convolution fusion | flops 404754432 | bytes 10485921 | tf_op jit(solution)/shard_map/while/body/eval_jaxpr/dot_general | solution.py:55
  72.1 2.6 fusion.36
  74.9 7.5 %convolution_add_fusion.2 = f32[64,16384]{1,0:T(8,128)} fusion(f32[64,16384]{1,0:T(8,128)} %get-tuple-element.234, f32[4,8,128,128]{3,2,1,0:T(8,128)S(1)} %bitcast.72, pred[]{:T(512)S(6)} %compare.3, s32[32]{0:T(128)S(1)} %dynamic_slice.54, pred[32]{0:T(512)(128)(4,1)S(1)} %dynamic_slice.55), kind=kOutput, calls=%fused_computation.2.clone.1 | convolution fusion | flops 404754432 | bytes 10485921 | tf_op jit(solution)/shard_map/while/body/eval_jaxpr/dot_general | solution.py:55
  85.2 7.5 %convolution_add_fusion.2 = f32[64,16384]{1,0:T(8,128)} fusion(f32[64,16384]{1,0:T(8,128)} %get-tuple-element.234, f32[4,8,128,128]{3,2,1,0:T(8,128)S(1)} %bitcast.72, pred[]{:T(512)S(6)} %compare.3, s32[32]{0:T(128)S(1)} %dynamic_slice.54, pred[32]{0:T(512)(128)(4,1)S(1)} %dynamic_slice.55), kind=kOutput, calls=%fused_computation.2.clone.1 | convolution fusion | flops 404754432 | bytes 10485921 | tf_op jit(solution)/shard_map/while/body/eval_jaxpr/dot_general | solution.py:55
  95.4 7.5 %convolution_add_fusion.2 = f32[64,16384]{1,0:T(8,128)} fusion(f32[64,16384]{1,0:T(8,128)} %get-tuple-element.234, f32[4,8,128,128]{3,2,1,0:T(8,128)S(1)} %bitcast.72, pred[]{:T(512)S(6)} %compare.3, s32[32]{0:T(128)S(1)} %dynamic_slice.54, pred[32]{0:T(512)(128)(4,1)S(1)} %dynamic_slice.55), kind=kOutput, calls=%fused_computation.2.clone.1 | convolution fusion | flops 404754432 | bytes 10485921 | tf_op jit(solution)/shard_map/while/body/eval_jaxpr/dot_general | solution.py:55
  102.9 2.7 fusion.36
  105.8 7.5 %convolution_add_fusion.2 = f32[64,16384]{1,0:T(8,128)} fusion(f32[64,16384]{1,0:T(8,128)} %get-tuple-element.234, f32[4,8,128,128]{3,2,1,0:T(8,128)S(1)} %bitcast.72, pred[]{:T(512)S(6)} %compare.3, s32[32]{0:T(128)S(1)} %dynamic_slice.54, pred[32]{0:T(512)(128)(4,1)S(1)} %dynamic_slice.55), kind=kOutput, calls=%fused_computation.2.clone.1 | convolution fusion | flops 404754432 | bytes 10485921 | tf_op jit(solution)/shard_map/while/body/eval_jaxpr/dot_general | solution.py:55
  113.3 2.6 fusion.36
  116.1 7.5 %convolution_add_fusion.2 = f32[64,16384]{1,0:T(8,128)} fusion(f32[64,16384]{1,0:T(8,128)} %get-tuple-element.234, f32[4,8,128,128]{3,2,1,0:T(8,128)S(1)} %bitcast.72, pred[]{:T(512)S(6)} %compare.3, s32[32]{0:T(128)S(1)} %dynamic_slice.54, pred[32]{0:T(512)(128)(4,1)S(1)} %dynamic_slice.55), kind=kOutput, calls=%fused_computation.2.clone.1 | convolution fusion | flops 404754432 | bytes 10485921 | tf_op jit(solution)/shard_map/while/body/eval_jaxpr/dot_general | solution.py:55
  123.6 2.9 %copy.65 = f32[8,8,128,128]{3,2,1,0:T(8,128)S(1)} copy(f32[8,8,128,128]{3,1,2,0:T(8,128)} %bitcast.73) | data formatting | bytes 8388608
  126.5 3.8 %fusion.24 = (f32[64,64,64]{2,1,0:T(8,128)}, f32[64,64,64]{2,1,0:T(8,128)}, f32[64,64,64]{2,1,0:T(8,128)}) fusion(f32[64,128,128]{2,1,0:T(8,128)S(1)} %bitcast.74), kind=kLoop, calls=%fused_computation.43 | loop fusion | bytes 6291456 | tf_op jit(solution)/shard_map/slice | solution.py:69
  132.7 4.2 %copy.61 = f32[64,64,64]{0,1,2:T(8,128)} copy(f32[64,64,64]{2,1,0:T(8,128)} %get-tuple-element.177) | data formatting | bytes 2097152
  136.8 4.2 %copy.63 = f32[64,64,64]{0,1,2:T(8,128)} copy(f32[64,64,64]{2,1,0:T(8,128)} %get-tuple-element.178) | data formatting | bytes 2097152
  146.5 6.4 %copy.53 = f32[64,1,129,64]{2,3,1,0:T(8,128)} copy(f32[64,1,129,64]{0,2,3,1:T(8,128)} %maximum_bitcast_fusion) | data formatting | bytes 4227072 | tf_op jit(solution)/shard_map/reshape | solution.py:14
  152.9 12.3 %all-to-all-start = ((f32[64,1,129,64]{2,3,1,0:T(8,128)}), f32[64,1,129,64]{2,3,1,0:T(8,128)}, u32[]{:S(2)}, u32[]{:S(2)}) async-start(f32[64,1,129,64]{2,3,1,0:T(8,128)} %copy.53), calls=%async_computation | async-start | bytes 8388608 | tf_op jit(solution)/shard_map/all_to_all | solution.py:20
  165.9 50.7 %all-to-all-done = f32[64,1,129,64]{2,3,1,0:T(8,128)} async-done(((f32[64,1,129,64]{2,3,1,0:T(8,128)}), f32[64,1,129,64]{2,3,1,0:T(8,128)}, u32[]{:S(2)}, u32[]{:S(2)}) %all-to-all-start) | async-done | bytes 2113568 | tf_op jit(solution)/shard_map/all_to_all | solution.py:20
  222.4 9.2 %all-reduce = f32[4]{0:T(128)S(1)} all-reduce(f32[4]{0:T(128)S(1)} %dynamic-update-slice), channel_id=1, replica_groups=mesh['sec_0'=4,'sec_1'=4,'sec_2'=4,'node'=2] {'sec_0'}, use_global_device_ids=true, to_apply=%add | all-reduce | flops 4 | bytes 32
  234.3 9.3 %all-reduce.1 = f32[4]{0:T(128)S(1)} all-reduce(f32[4]{0:T(128)S(1)} %dynamic-update-slice.1), channel_id=1, replica_groups=mesh['sec_0'=4,'sec_1'=4,'sec_2'=4,'node'=2] {'sec_1'}, use_global_device_ids=true, to_apply=%add.1 | all-reduce | flops 4 | bytes 32
  246.4 7.0 %all-reduce.2 = f32[4]{0:T(128)S(1)} all-reduce(f32[4]{0:T(128)S(1)} %dynamic-update-slice.2), channel_id=1, replica_groups=mesh['sec_0'=4,'sec_1'=4,'sec_2'=4,'node'=2] {'sec_2'}, use_global_device_ids=true, to_apply=%add.2 | all-reduce | flops 4 | bytes 32
  255.5 9.9 %all-reduce.3 = f32[2]{0:T(128)S(1)} all-reduce(f32[2]{0:T(128)S(1)} %dynamic-update-slice.3), channel_id=1, replica_groups=mesh['sec_0'=4,'sec_1'=4,'sec_2'=4,'node'=2] {'node'}, use_global_device_ids=true, to_apply=%add.3 | all-reduce | flops 2 | bytes 16
  (78 shorter events, 36.8 us)
Async XLA Ops:
  141.9 2.2 copy-start
  152.9 12.4 %copy-start.4 = (u32[128]{0:T(128)S(1)}, u32[128]{0:T(128)}, u32[]{:S(2)}) copy-start(u32[128]{0:T(128)} %constant.91) | copy-start | bytes 1540
  152.9 63.7 %all-to-all-start = ((f32[64,1,129,64]{2,3,1,0:T(8,128)}), f32[64,1,129,64]{2,3,1,0:T(8,128)}, u32[]{:S(2)}, u32[]{:S(2)}) async-start(f32[64,1,129,64]{2,3,1,0:T(8,128)} %copy.53), calls=%async_computation | async-start | bytes 8388608 | tf_op jit(solution)/shard_map/all_to_all | solution.py:20
  165.2 56.5 %copy-start.3 = (u32[128]{0:T(128)S(1)}, u32[128]{0:T(128)}, u32[]{:S(2)}) copy-start(u32[128]{0:T(128)} %constant.96) | copy-start | bytes 1540
  165.2 68.4 %copy-start.2 = (u32[128]{0:T(128)S(1)}, u32[128]{0:T(128)}, u32[]{:S(2)}) copy-start(u32[128]{0:T(128)} %constant.101) | copy-start | bytes 1540
  165.3 80.5 %copy-start.1 = (u32[128]{0:T(128)S(1)}, u32[128]{0:T(128)}, u32[]{:S(2)}) copy-start(u32[128]{0:T(128)} %constant.106) | copy-start | bytes 1540
